TPU v7x, 32 devices: a whole 2x2x4 slice. The times are simulated.
32 devices in a mesh: ctx: 4 (over y, x), fsdp: 8 (over z, core).
Axes of the slice: x: 2, y: 2, z: 4, core: 2. Of those that a mesh axis runs over, the one named last changes fastest.
Arguments:
- layer_input: bfloat16 [1280, 4, 1536], P(('ctx', 'fsdp')), may hold values from -6 to 6
- block_order: int32 [2, 8], replicated, may hold values from 0 to 7, each once within a row
- first_gain: bfloat16 [1536], P('fsdp'), may hold values from 0.25 to 1.75
- w_qkv: bfloat16 [1536, 2048], P('fsdp'), may hold values from -0.15625 to 0.15625
- b_qkv: bfloat16 [2048], P('fsdp'), may hold values from -1.5 to 1.5
- w_o: bfloat16 [1536, 1536], P('fsdp'), may hold values from -1.25 to 1.25
- second_gain: bfloat16 [1536], P('fsdp'), may hold values from 0.25 to 1.75
- w_gate: bfloat16 [1536, 8960], P('fsdp'), may hold values from -0.15625 to 0.15625
- w_up: bfloat16 [1536, 8960], P('fsdp'), may hold values from -0.15625 to 0.15625
- w_down: bfloat16 [8960, 1536], P('fsdp'), may hold values from -0.0625 to 0.0625
- cotangent: bfloat16 [1280, 4, 1536], P(('ctx', 'fsdp')), may hold values from -6 to 6
Outputs:
- mixed: bfloat16 [1280, 4, 1536], P(('ctx', 'fsdp'))
- input_grad: float32 [1280, 4, 1536], P(('ctx', 'fsdp'))
- first_gain_grad: float32 [1536], P('fsdp')
- w_qkv_grad: float32 [1536, 2048], P('fsdp')
- b_qkv_grad: float32 [1792], P('fsdp')
- value_bias_grad: float32 [256], P('fsdp')
- w_o_grad: float32 [1536, 1536], P('fsdp')
- second_gain_grad: float32 [1536], P('fsdp')
- w_gate_grad: float32 [1536, 8960], P('fsdp')
- w_up_grad: float32 [1536, 8960], P('fsdp')
- w_down_grad: float32 [8960, 1536], P('fsdp')
Inputs may be any that keep to these rules, and one draw needn't show every extreme that they name: `block_order`: each row is a permutation.
All inputs are finite; a program needn't handle non-finite values.
Results may differ from a plain program's by a relative error of at most 0.02.
Values may be sent and summed in bfloat16 or wider, within the bound.
A program may use at most 576 MiB of HBM per device.

v0:
```python
import math
import jax
import jax.numpy as jnp
from jax import lax
from jax.sharding import PartitionSpec as P

D = 1536
H = 12
KVH = 2
HD = 128
FF = 8960
SEQS = 2
QKV = 2048
QK = 1792
EPS = 1e-06
THETA = 1000000.0
KEY_BLOCK = 256
NEG_FILL = -1e30
CONTRACT_LAST = (((1,), (1,)), ((), ()))
CONTRACT_FIRST = (((0,), (0,)), ((), ()))


def narrowed(values):
    return lax.optimization_barrier(values.astype(jnp.bfloat16)).astype(jnp.float32)


def block_positions(block_order, first_row, row_count, block_rows, ctx_size):
    row_index = first_row + jnp.arange(row_count, dtype=jnp.int32)
    slot_index = jnp.arange(2 * SEQS, dtype=jnp.int32)
    entries = (slot_index // SEQS)[None, :] * ctx_size + (row_index // block_rows)[:, None]
    tiled = jnp.tile(block_order, (2, 1))
    entry_ids = jnp.arange(2 * ctx_size, dtype=jnp.int32)
    picked = jnp.sum(
        jnp.where(entries[:, :, None] == entry_ids[None, None, :], tiled[None, :, :], 0), -1
    )
    return picked * block_rows + (row_index % block_rows)[:, None]


def pos_groups(positions):
    row_count = positions.shape[0]
    return positions.reshape(row_count, 2, SEQS).transpose(2, 0, 1).reshape(SEQS, row_count * 2)


def to_groups(tokens, row_count, group_size):
    shaped = tokens.reshape(row_count, 2, SEQS, KVH, group_size, HD)
    return shaped.transpose(2, 3, 4, 0, 1, 5).reshape(SEQS, KVH, group_size * row_count * 2, HD)


def from_groups(grouped, row_count, group_size):
    shaped = grouped.reshape(SEQS, KVH, group_size, row_count, 2, HD).transpose(3, 4, 0, 1, 2, 5)
    return shaped.reshape(row_count * 2 * SEQS, KVH * group_size * HD)


def rope_tables(positions):
    half_width = HD // 2
    frequency = THETA ** (-jnp.arange(half_width, dtype=jnp.float32) * 2.0 / HD)
    angles = positions.astype(jnp.float32)[:, None] * frequency[None, :]
    cosine_table = jnp.concatenate([jnp.cos(angles), jnp.cos(angles)], -1)[:, None, :]
    sine_table = jnp.concatenate([jnp.sin(angles), jnp.sin(angles)], -1)[:, None, :]
    return (cosine_table, sine_table)


def rotate(head_values, cosine_table, sine_table):
    half_width = HD // 2
    turned = jnp.concatenate([-head_values[..., half_width:], head_values[..., :half_width]], -1)
    return head_values * cosine_table + turned * sine_table


def rotate_back(grad_values, cosine_table, sine_table):
    half_width = HD // 2
    moved = grad_values * sine_table
    return grad_values * cosine_table + jnp.concatenate(
        [moved[..., half_width:], -moved[..., :half_width]], -1
    )


def normalize(values, gain):
    scale = lax.rsqrt(jnp.mean(values * values, -1, keepdims=True) + EPS)
    unit = values * scale
    return (unit, scale, unit * gain)


def norm_back(grad_out, unit, scale, gain):
    grad_unit = grad_out * gain
    inner = jnp.mean(grad_unit * unit, -1, keepdims=True)
    return (scale * (grad_unit - unit * inner), jnp.sum(grad_out * unit, 0))


def split_blocks(piece):
    row_count = piece.shape[0]
    size = math.gcd(row_count, KEY_BLOCK)
    stacked = piece.reshape(row_count // size, size, piece.shape[1], piece.shape[2])
    firsts = size * jnp.arange(row_count // size, dtype=jnp.int32)
    return (stacked, firsts)


def shards(
    layer_input,
    block_order,
    first_gain,
    w_qkv,
    b_qkv,
    w_o,
    second_gain,
    w_gate,
    w_up,
    w_down,
    cotangent,
):
    ctx_size = lax.axis_size("ctx")
    shard_count = lax.axis_size("fsdp")
    rows_here = layer_input.shape[0]
    slots = layer_input.shape[1]
    block_rows = rows_here * shard_count
    group_size = H // KVH
    kv_width = KVH * HD
    first_row = (lax.axis_index("ctx") * shard_count + lax.axis_index("fsdp")) * rows_here
    own_pos = block_positions(block_order, first_row, rows_here, block_rows, ctx_size)
    cosine_table, sine_table = rope_tables(own_pos.reshape(-1))
    query_scale = HD ** (-0.5)
    w_qkv_all, w_o_all, bias_all, gain_one, gain_two = (
        lax.all_gather(w_qkv, "fsdp", axis=0, tiled=True),
        lax.all_gather(w_o, "fsdp", axis=0, tiled=True),
        lax.all_gather(b_qkv, "fsdp", axis=0, tiled=True),
        lax.all_gather(first_gain, "fsdp", axis=0, tiled=True),
        lax.all_gather(second_gain, "fsdp", axis=0, tiled=True),
    )
    gain_one = gain_one.astype(jnp.float32)
    gain_two = gain_two.astype(jnp.float32)
    inputs = layer_input.reshape(-1, D).astype(jnp.float32)
    unit_one, scale_one, normed = normalize(inputs, gain_one)
    normed_one = normed.astype(jnp.bfloat16)
    projected = jnp.dot(
        normed_one, w_qkv_all, preferred_element_type=jnp.float32
    ) + bias_all.astype(jnp.float32)
    query_raw = projected[:, : H * HD].reshape(-1, H, HD)
    key_raw = projected[:, H * HD : H * HD + kv_width].reshape(-1, KVH, HD)
    value_raw = projected[:, H * HD + kv_width :]
    query_tokens = (
        (rotate(query_raw, cosine_table, sine_table) * query_scale)
        .astype(jnp.bfloat16)
        .reshape(-1, H * HD)
    )
    key_tokens = (
        rotate(key_raw, cosine_table, sine_table).astype(jnp.bfloat16).reshape(-1, kv_width)
    )
    own_kv = jnp.concatenate([key_tokens, value_raw.astype(jnp.bfloat16)], -1).reshape(
        rows_here, slots, 2 * kv_width
    )
    block_kv = lax.all_gather(own_kv, "fsdp", axis=0, tiled=True)
    queries = to_groups(query_tokens, rows_here, group_size)
    query_pos = jnp.tile(pos_groups(own_pos), (1, group_size))
    query_count = queries.shape[2]

    def piece_keys(key_rows, row_start):
        row_count = key_rows.shape[0]
        flat = key_rows.reshape(row_count * slots, 2 * kv_width)
        keys_grouped = to_groups(flat[:, :kv_width], row_count, 1)
        values_grouped = to_groups(flat[:, kv_width:], row_count, 1)
        key_pos = pos_groups(
            block_positions(block_order, row_start, row_count, block_rows, ctx_size)
        )
        visible = query_pos[:, None, :, None] >= key_pos[:, None, None, :]
        scores = jnp.einsum(
            "snmd,snkd->snmk", queries, keys_grouped, preferred_element_type=jnp.float32
        )
        return (keys_grouped, values_grouped, visible, scores)

    start_state = (
        jnp.full((SEQS, KVH, query_count), NEG_FILL, jnp.float32),
        jnp.zeros((SEQS, KVH, query_count), jnp.float32),
        jnp.zeros((SEQS, KVH, query_count, HD), jnp.float32),
    )
    state = start_state
    stacked, firsts = split_blocks(lax.all_gather(block_kv, "ctx", axis=0, tiled=True))

    def forward_one_block(carry, item):
        best, totals, accum = carry
        key_rows, row_start = item
        keys_grouped, values_grouped, visible, scores = piece_keys(key_rows, row_start)
        scores = jnp.where(visible, scores, NEG_FILL)
        fresh = jnp.maximum(best, jnp.max(scores, -1))
        weights = jnp.where(visible, jnp.exp(scores - fresh[..., None]), 0.0)
        decay = jnp.exp(best - fresh)
        totals = totals * decay + jnp.sum(weights, -1)
        accum = accum * decay[..., None] + jnp.einsum(
            "snmk,snkd->snmd",
            weights.astype(jnp.bfloat16),
            values_grouped,
            preferred_element_type=jnp.float32,
        )
        return ((fresh, totals, accum), None)

    state, unused = lax.scan(forward_one_block, state, (stacked, firsts))
    best, totals, accum = state
    attended_grouped = accum / totals[..., None]
    logsum = best + jnp.log(totals)
    attended_low = from_groups(attended_grouped, rows_here, group_size).astype(jnp.bfloat16)
    middle = inputs + jnp.dot(attended_low, w_o_all, preferred_element_type=jnp.float32)
    unit_two, scale_two, normed = normalize(middle, gain_two)
    normed_two = normed.astype(jnp.bfloat16)
    gate_all, up_all, down_all = (
        lax.all_gather(w_gate, "fsdp", axis=0, tiled=True),
        lax.all_gather(w_up, "fsdp", axis=0, tiled=True),
        lax.all_gather(w_down, "fsdp", axis=0, tiled=True),
    )
    gate_part = jnp.dot(normed_two, gate_all, preferred_element_type=jnp.float32)
    up_part = jnp.dot(normed_two, up_all, preferred_element_type=jnp.float32)
    activated = jax.nn.silu(gate_part)
    hidden = (activated * up_part).astype(jnp.bfloat16)
    mixed_out = middle + jnp.dot(hidden, down_all, preferred_element_type=jnp.float32)
    output = mixed_out.astype(jnp.bfloat16).reshape(rows_here, slots, D)
    gate_all, up_all, down_all = (
        lax.all_gather(w_gate, "fsdp", axis=0, tiled=True),
        lax.all_gather(w_up, "fsdp", axis=0, tiled=True),
        lax.all_gather(w_down, "fsdp", axis=0, tiled=True),
    )
    w_qkv_all, w_o_all = (
        lax.all_gather(w_qkv, "fsdp", axis=0, tiled=True),
        lax.all_gather(w_o, "fsdp", axis=0, tiled=True),
    )
    grad_branch_two = cotangent.reshape(-1, D)
    grad_hidden = lax.dot_general(
        grad_branch_two, down_all, CONTRACT_LAST, preferred_element_type=jnp.float32
    )
    sigmoid_gate = jax.nn.sigmoid(gate_part)
    grad_gate = grad_hidden * up_part * sigmoid_gate * (1.0 + gate_part * (1.0 - sigmoid_gate))
    grad_gate_up = jnp.concatenate([grad_gate, grad_hidden * activated], -1).astype(jnp.bfloat16)
    grad_normed_two = lax.dot_general(
        grad_gate_up[:, :FF], gate_all, CONTRACT_LAST, preferred_element_type=jnp.float32
    )
    grad_normed_two = grad_normed_two + lax.dot_general(
        grad_gate_up[:, FF:], up_all, CONTRACT_LAST, preferred_element_type=jnp.float32
    )
    grad_middle_norm, grad_gain_two = norm_back(grad_normed_two, unit_two, scale_two, gain_two)
    grad_middle = cotangent.reshape(-1, D).astype(jnp.float32) + grad_middle_norm
    grad_branch_one = grad_middle.astype(jnp.bfloat16)
    grad_attended = lax.dot_general(
        grad_branch_one, w_o_all, CONTRACT_LAST, preferred_element_type=jnp.float32
    ).astype(jnp.bfloat16)
    grad_out_grouped = to_groups(grad_attended, rows_here, group_size)
    delta = jnp.sum(grad_out_grouped.astype(jnp.float32) * attended_grouped, -1)
    back_state = (
        jnp.zeros((SEQS, KVH, query_count, HD), jnp.float32),
        jnp.zeros((ctx_size * block_rows, slots, 2 * kv_width), jnp.float32),
    )
    state = back_state
    stacked, firsts = split_blocks(lax.all_gather(block_kv, "ctx", axis=0, tiled=True))

    def backward_one_block(carry, item):
        grad_queries, grad_kv_full = carry
        key_rows, row_start = item
        row_count = key_rows.shape[0]
        keys_grouped, values_grouped, visible, scores = piece_keys(key_rows, row_start)
        probs = jnp.where(
            visible, jnp.exp(jnp.where(visible, scores, NEG_FILL) - logsum[..., None]), 0.0
        )
        grad_probs = jnp.einsum(
            "snmd,snkd->snmk", grad_out_grouped, values_grouped, preferred_element_type=jnp.float32
        )
        grad_scores = (probs * (grad_probs - delta[..., None])).astype(jnp.bfloat16)
        grad_queries = grad_queries + jnp.einsum(
            "snmk,snkd->snmd", grad_scores, keys_grouped, preferred_element_type=jnp.float32
        )
        grad_keys = jnp.einsum(
            "snmk,snmd->snkd", grad_scores, queries, preferred_element_type=jnp.float32
        )
        grad_values = jnp.einsum(
            "snmk,snmd->snkd",
            probs.astype(jnp.bfloat16),
            grad_out_grouped,
            preferred_element_type=jnp.float32,
        )
        block_terms = jnp.concatenate(
            [from_groups(grad_keys, row_count, 1), from_groups(grad_values, row_count, 1)], -1
        ).reshape(row_count, slots, 2 * kv_width)
        previous = lax.dynamic_slice_in_dim(grad_kv_full, row_start, row_count, 0)
        grad_kv_full = lax.dynamic_update_slice_in_dim(
            grad_kv_full, previous + block_terms, row_start, 0
        )
        return ((grad_queries, grad_kv_full), None)

    state, unused = lax.scan(backward_one_block, state, (stacked, firsts))
    grad_queries, grad_kv_full = state
    grad_kv = lax.psum_scatter(grad_kv_full, ("ctx", "fsdp"), scatter_dimension=0, tiled=True)
    grad_kv_low = narrowed(grad_kv).reshape(-1, 2 * kv_width)
    grad_query_tokens = from_groups(narrowed(grad_queries), rows_here, group_size) * query_scale
    grad_query_raw = rotate_back(
        grad_query_tokens.reshape(-1, H, HD), cosine_table, sine_table
    ).reshape(-1, H * HD)
    grad_key_raw = rotate_back(
        grad_kv_low[:, :kv_width].reshape(-1, KVH, HD), cosine_table, sine_table
    ).reshape(-1, kv_width)
    grad_projected = jnp.concatenate(
        [grad_query_raw, grad_key_raw, grad_kv_low[:, kv_width:]], -1
    ).astype(jnp.bfloat16)
    grad_bias = jnp.sum(grad_projected, 0, dtype=jnp.float32)
    grad_bias_qk = grad_bias[:QK]
    grad_bias_value = grad_bias[QK:]
    grad_normed_one = lax.dot_general(
        grad_projected, w_qkv_all, CONTRACT_LAST, preferred_element_type=jnp.float32
    )
    grad_input_norm, grad_gain_one = norm_back(grad_normed_one, unit_one, scale_one, gain_one)
    grad_input = (grad_middle + grad_input_norm).reshape(rows_here, slots, D)
    weight_rows = lax.psum_scatter(
        jnp.concatenate(
            [
                lax.dot_general(
                    normed_two, grad_gate_up, CONTRACT_FIRST, preferred_element_type=jnp.float32
                ),
                lax.dot_general(
                    normed_one, grad_projected, CONTRACT_FIRST, preferred_element_type=jnp.float32
                ),
                lax.dot_general(
                    attended_low,
                    grad_branch_one,
                    CONTRACT_FIRST,
                    preferred_element_type=jnp.float32,
                ),
            ],
            1,
        ).astype(jnp.bfloat16),
        "fsdp",
        scatter_dimension=0,
        tiled=True,
    ).astype(jnp.float32)
    down_rows = lax.psum_scatter(
        lax.dot_general(
            hidden, grad_branch_two, CONTRACT_FIRST, preferred_element_type=jnp.float32
        ).astype(jnp.bfloat16),
        "fsdp",
        scatter_dimension=0,
        tiled=True,
    ).astype(jnp.float32)
    gain_one_rows, gain_two_rows, bias_rows, value_bias_rows = (
        lax.psum_scatter(grad_gain_one, "fsdp", scatter_dimension=0, tiled=True),
        lax.psum_scatter(grad_gain_two, "fsdp", scatter_dimension=0, tiled=True),
        lax.psum_scatter(grad_bias_qk, "fsdp", scatter_dimension=0, tiled=True),
        lax.psum_scatter(grad_bias_value, "fsdp", scatter_dimension=0, tiled=True),
    )
    weight_rows, down_rows, gain_one_rows, gain_two_rows, bias_rows, value_bias_rows = (
        lax.psum(weight_rows.astype(jnp.bfloat16), "ctx").astype(jnp.float32),
        lax.psum(down_rows.astype(jnp.bfloat16), "ctx").astype(jnp.float32),
        lax.psum(gain_one_rows.astype(jnp.bfloat16), "ctx").astype(jnp.float32),
        lax.psum(gain_two_rows.astype(jnp.bfloat16), "ctx").astype(jnp.float32),
        lax.psum(bias_rows.astype(jnp.bfloat16), "ctx").astype(jnp.float32),
        lax.psum(value_bias_rows.astype(jnp.bfloat16), "ctx").astype(jnp.float32),
    )
    return (
        output,
        grad_input,
        gain_one_rows,
        weight_rows[:, 2 * FF : 2 * FF + QKV],
        bias_rows,
        value_bias_rows,
        weight_rows[:, 2 * FF + QKV :],
        gain_two_rows,
        weight_rows[:, :FF],
        weight_rows[:, FF : 2 * FF],
        down_rows,
    )


def solution(mesh):
    in_specs = (
        P(("ctx", "fsdp"), None, None),
        P(),
        P("fsdp"),
        P("fsdp", None),
        P("fsdp"),
        P("fsdp", None),
        P("fsdp"),
        P("fsdp", None),
        P("fsdp", None),
        P("fsdp", None),
        P(("ctx", "fsdp"), None, None),
    )
    out_specs = (
        P(("ctx", "fsdp"), None, None),
        P(("ctx", "fsdp"), None, None),
        P("fsdp"),
        P("fsdp", None),
        P("fsdp"),
        P("fsdp"),
        P("fsdp", None),
        P("fsdp"),
        P("fsdp", None),
        P("fsdp", None),
        P("fsdp", None),
    )
    return jax.shard_map(shards, mesh=mesh, in_specs=in_specs, out_specs=out_specs, check_vma=False)
```

profile of v0, /device:TPU:0, one launch (start us, length us, event | category | flops | bytes accessed | tf_op | source)
XLA Modules:
  0.0 2331.6 jit_solution(8139246037101609936)
XLA Ops:
  9.8 13.5 all-gather
  27.0 15.6 all-reduce.8
  46.4 31.2 %all-gather.9.cloned.1.call-done = bf16[1536,2048]{1,0:T(8,128)(2,1)} async-done(((bf16[192,2048]{1,0:T(8,128)(2,1)}), bf16[1536,2048]{1,0:T(8,128)(2,1)}) %all-gather.9.cloned.1.call-update) | async-done | bytes 6291472 | tf_op jit(solution)/shard_map/all_gather | solution.py:122
  77.6 4.0 convolution_add_fusion.4
  84.0 22.2 all-gather.11.cloned.1.call-done
  125.7 43.1 %all-gather.13.cloned.1.call-done = bf16[1280,4,512]{2,1,0:T(4,128)(2,1)} async-done(((bf16[320,4,512]{2,1,0:T(4,128)(2,1)}), bf16[1280,4,512]{2,1,0:T(4,128)(2,1)}) %all-gather.13.cloned.1.call-update) | async-done | bytes 5242896 | tf_op jit(solution)/shard_map/all_gather | solution.py:175
  168.8 82.5 %while.34 = (s32[]{:T(128)}, f32[2,2,480]{2,1,0:T(2,128)S(1)}, f32[2,2,480]{2,1,0:T(2,128)S(1)}, f32[2,2,480,128]{3,2,1,0:T(8,128)}, s32[5]{0:T(128)S(1)}, /*ind...) while((s32[]{:T(128)}, f32[2,2,480]{2,1,0:T(2,128)S(1)}, ...), condition=%wide.region_6.7_spmd.clone, body=%wide.region_2.6_spmd.clone.sunk | while | flops 514415264 | bytes 27955316 | solution.py:194
  176.3 3.8 fusion.144
  180.6 4.4 fusion.146
  196.7 4.7 fusion.146
  213.0 4.7 fusion.146
  229.2 5.5 fusion.146
  246.4 4.7 fusion.146
  257.4 203.6 %all-gather.17.cloned.1.call-done = bf16[1536,8960]{1,0:T(8,128)(2,1)} async-done(((bf16[192,8960]{1,0:T(8,128)(2,1)}), bf16[1536,8960]{1,0:T(8,128)(2,1)}) %all-gather.17.cloned.1.call-update) | async-done | bytes 27525136 | tf_op jit(solution)/shard_map/all_gather | solution.py:203
  461.0 16.3 fusion.69
  477.3 222.6 %all-gather.19.cloned.1.call-done = bf16[1536,8960]{1,0:T(8,128)(2,1)} async-done(((bf16[192,8960]{1,0:T(8,128)(2,1)}), bf16[1536,8960]{1,0:T(8,128)(2,1)}) %all-gather.19.cloned.1.call-update) | async-done | bytes 27525136 | tf_op jit(solution)/shard_map/all_gather | solution.py:204
  699.9 16.4 fusion.70
  716.4 222.6 %all-gather.21.cloned.1.call-done = bf16[8960,1536]{1,0:T(8,128)(2,1)} async-done(((bf16[1120,1536]{1,0:T(8,128)(2,1)}), bf16[8960,1536]{1,0:T(8,128)(2,1)}) %all-gather.21.cloned.1.call-update) | async-done | bytes 27525136 | tf_op jit(solution)/shard_map/all_gather | solution.py:205
  939.0 19.8 multiply_convert_fusion
  958.8 15.2 convolution_convert_fusion.1
  974.0 17.0 fusion.71
  991.0 16.1 multiply_reduce_fusion
  1008.4 4.1 convolution_convert_fusion.4
  1014.9 4.9 broadcast_in_dim.152
  1019.8 165.6 %while.35 = (s32[]{:T(128)}, f32[2,2,480,128]{3,2,1,0:T(8,128)}, f32[1280,4,512]{2,1,0:T(4,128)}, s32[5]{0:T(128)S(1)}, s32[2,8]{1,0:T(2,128)S(1)}, /*index=5*/b...) while((s32[]{:T(128)}, f32[2,2,480,128]{3,2,1,0:T(8,128)}, ...), condition=%wide.region_12.13_spmd.clone, body=%wide.region_10.12_spmd.clone.sunk | while | flops 1270183168 | bytes 55970532 | solution.py:283
  1027.9 4.0 fusion.160
  1035.5 3.8 fusion.161
  1059.9 4.0 fusion.160
  1068.7 3.8 fusion.161
  1093.0 3.9 fusion.160
  1101.8 4.2 fusion.161
  1126.6 3.9 fusion.160
  1135.4 3.9 fusion.161
  1159.9 3.9 fusion.160
  1168.7 3.8 fusion.161
  1181.4 3.7 fusion.163
  1188.1 176.6 %all-reduce.15 = bf16[1280,4,512]{2,1,0:T(4,128)(2,1)} all-reduce(f32[1280,4,512]{2,1,0:T(4,128)} %get-tuple-element.344), channel_id=2, replica_groups=mesh['ctx'=4,'fsdp'=8] {'ctx','fsdp'}, use_global_device_ids=true, to_apply=%region_13.14.clone | all-reduce | flops 2621440 | bytes 15728640
  1376.0 4.6 convolution_convert_fusion.2
  1380.7 23.8 %convolution_convert_fusion = bf16[1536,17920]{1,0:T(8,128)(2,1)} fusion(bf16[160,1536]{1,0:T(8,128)(2,1)S(1)} %copy-done.10, bf16[160,8960]{1,0:T(8,128)(2,1)} %get-tuple-element.485, bf16[160,8960]{1,0:T(8,128)(2,1)} %get-tuple-element.486), kind=kOutput, calls=%fused_computation.72 | convolution fusion | flops 8847032320 | bytes 61276160 | tf_op jit(solution)/shard_map/dot_general | solution.py:308
  1404.5 44.2 %pad_maximum_fusion = bf16[1536,21504]{1,0:T(8,128)(2,1)} fusion(bf16[1536,1536]{1,0:T(8,128)(2,1)} %convolution_convert_fusion.3, bf16[1536,2048]{1,0:T(8,128)(2,1)} %convolution_convert_fusion.2, bf16[1536,17920]{1,0:T(8,128)(2,1)} %convolution_convert_fusion), kind=kLoop, calls=%fused_computation.73 | loop fusion | flops 198180864 | bytes 132120576 | tf_op jit(solution)/shard_map/concatenate | solution.py:306
  1448.8 629.6 %reduce-scatter.3.cloned.1.call-done = bf16[192,21504]{1,0:T(8,128)(2,1)} async-done(((bf16[1536,21504]{1,0:T(8,128)(2,1)}), bf16[192,21504]{1,0:T(8,128)(2,1)}) %reduce-scatter.3.cloned.1.call-update) | async-done | bytes 8257552 | tf_op jit(solution)/shard_map/reduce_scatter | solution.py:305
  2080.4 16.4 fusion.44
  2098.7 5.7 multiply_reduce_fusion.1
  2107.0 26.1 %all-reduce.7 = (bf16[1536]{0:T(1024)(128)(2,1)S(1)}, bf16[1792]{0:T(1024)(128)(2,1)S(1)}, bf16[256]{0:T(256)(128)(2,1)S(1)}, bf16[1536]{0:T(1024)(128)(2,1)S(1)}) all-reduce(f32[1536]{0:T(1024)S(1)} %get-tuple-element.419, f32[1792]{0:T(1024)S(1)} %bitcast.253, ...), channel_id=3, replica_groups=mesh['ctx'=4,'fsdp'=8] {'fsdp'}, use_global_device_ids=true, to_apply=%region_16.17.clone | all-reduce | flops 5120 | bytes 30720
  2133.4 10.2 all-reduce.9
  2145.9 160.7 %all-reduce.14.cloned.1.call-done = (bf16[192,21504]{1,0:T(8,128)(2,1)}, bf16[1120,1536]{1,0:T(8,128)(2,1)}) async-done(((bf16[192,21504]{1,0:T(8,128)(2,1)}, bf16[1120,1536]{1,0:T(8,128)(2,1)}), (bf16[192,21504]{1,0:T(8,128)(2,1)}, bf16[1120,1536]{1,0:T(8,128)(2,1)})) %all-reduce.14.cloned.1.call-update) | async-done | bytes 11698192 | tf_op jit(solution)/shard_map/psum | solution.py:342
  2311.2 9.2 fusion.62
  2320.5 3.9 convert_element_type.184
  (488 shorter events, 231.9 us)
Async XLA Ops:
  7.2 70.4 %all-gather.9.cloned.1.call-start = ((), (), s32[]{:S(2)}) async-start(), calls=%async_computation.2 | async-start | bytes 7077888 | tf_op jit(solution)/shard_map/all_gather | solution.py:122
  7.9 98.2 %all-gather.11.cloned.1.call-start = ((), (), s32[]{:S(2)}) async-start(), calls=%async_computation.3 | async-start | bytes 1474560 | tf_op jit(solution)/shard_map/all_gather | solution.py:150
  9.1 72.6 %copy-start = (f32[160,1536]{1,0:T(8,128)}, f32[160,1536]{1,0:T(8,128)S(1)}, u32[]{:S(2)}) copy-start(f32[160,1536]{1,0:T(8,128)S(1)} %reshape.608) | copy-start | bytes 2949124
  42.6 39.1 %copy-start.29 = (f32[1536]{0:T(1024)}, f32[1536]{0:T(1024)S(1)}, u32[]{:S(2)}) copy-start(f32[1536]{0:T(1024)S(1)} %convert_element_type.151) | copy-start | bytes 18436
  44.1 33.6 %copy-start.32 = (f32[160]{0:T(256)}, f32[160]{0:T(256)S(1)}, u32[]{:S(2)}) copy-start(f32[160]{0:T(256)S(1)} %rsqrt.20) | copy-start | bytes 1924
  45.6 36.7 %copy-start.26 = (f32[160,128]{1,0:T(8,128)}, f32[160,128]{1,0:T(8,128)S(1)}, u32[]{:S(2)}) copy-start(f32[160,128]{1,0:T(8,128)S(1)} %pad_maximum_fusion.4) | copy-start | bytes 245764
  46.4 35.7 %copy-start.24 = (f32[160,128]{1,0:T(8,128)}, f32[160,128]{1,0:T(8,128)S(1)}, u32[]{:S(2)}) copy-start(f32[160,128]{1,0:T(8,128)S(1)} %get-tuple-element.501) | copy-start | bytes 245764
  81.7 25.7 %copy-start.13 = (f32[160,2048]{1,0:T(8,128)}, f32[160,2048]{1,0:T(8,128)S(1)}, u32[]{:S(2)}) copy-start(f32[160,2048]{1,0:T(8,128)S(1)} %convolution_add_fusion.4) | copy-start | bytes 3932164
  83.9 84.9 %all-gather.13.cloned.1.call-start = ((), (), s32[]{:S(2)}) async-start(), calls=%async_computation.4 | async-start | bytes 6553600 | tf_op jit(solution)/shard_map/all_gather | solution.py:175
  106.1 147.5 %all-gather.15.cloned.1.call-start = ((), (), s32[]{:S(2)}) async-start(), calls=%async_computation.5 | async-start | bytes 5308416 | tf_op jit(solution)/shard_map/all_gather | solution.py:123
  106.7 354.3 %all-gather.17.cloned.1.call-start = ((), (), s32[]{:S(2)}) async-start(), calls=%async_computation.6 | async-start | bytes 30965760 | tf_op jit(solution)/shard_map/all_gather | solution.py:203
  107.3 1.9 copy-start.28
  107.3 592.6 %all-gather.19.cloned.1.call-start = ((), (), s32[]{:S(2)}) async-start(), calls=%async_computation.7 | async-start | bytes 30965760 | tf_op jit(solution)/shard_map/all_gather | solution.py:204
  107.4 5.0 copy-start.14
  107.9 831.1 %all-gather.21.cloned.1.call-start = ((), (), s32[]{:S(2)}) async-start(), calls=%async_computation.8 | async-start | bytes 30965760 | tf_op jit(solution)/shard_map/all_gather | solution.py:205
  108.7 1340.1 %reduce-scatter.5.cloned.1.call-start = ((), (), s32[]{:S(2)}) async-start(), calls=%async_computation.10 | async-start | bytes 30965760 | tf_op jit(solution)/shard_map/reduce_scatter | solution.py:327
  116.4 7.4 copy-start.15
  122.0 46.8 %copy-start.31 = (s32[2,8]{1,0:T(2,128)S(1)}, s32[2,8]{1,0:T(2,128)}, u32[]{:S(2)}) copy-start(s32[2,8]{1,0:T(2,128)} %param.16) | copy-start | bytes 196
  251.3 2.4 copy-start.1
  253.7 3.8 copy-start.11
  257.2 749.9 %copy-start.7 = (f32[160,1536]{1,0:T(8,128)}, f32[160,1536]{1,0:T(8,128)S(1)}, u32[]{:S(2)}) copy-start(f32[160,1536]{1,0:T(8,128)S(1)} %get-tuple-element.513) | copy-start | bytes 2949124
  257.4 442.5 %copy-start.9 = (bf16[160,1536]{1,0:T(8,128)(2,1)}, bf16[160,1536]{1,0:T(8,128)(2,1)S(1)}, u32[]{:S(2)}) copy-start(bf16[160,1536]{1,0:T(8,128)(2,1)S(1)} %multiply_convert_fusion.3) | copy-start | bytes 1474564
  477.3 461.7 %copy-start.16 = (bf16[160,1536]{1,0:T(8,128)(2,1)S(1)}, bf16[160,1536]{1,0:T(8,128)(2,1)}, u32[]{:S(2)}) copy-start(bf16[160,1536]{1,0:T(8,128)(2,1)} %reshape.600) | copy-start | bytes 1474564
  974.0 1104.4 %reduce-scatter.3.cloned.1.call-start = ((), (), s32[]{:S(2)}) async-start(), calls=%async_computation.9 | async-start | bytes 74317824 | tf_op jit(solution)/shard_map/reduce_scatter | solution.py:305
  1008.4 5.8 copy-start.17
  1027.9 4.0 copy-start.5
  1031.9 3.6 copy-start.6
  1059.9 4.0 copy-start.5
  1063.8 4.9 copy-start.6
  1093.0 3.9 copy-start.5
  1096.9 4.9 copy-start.6
  1126.6 3.9 copy-start.5
  1130.5 4.9 copy-start.6
  1159.8 3.9 copy-start.5
  1163.8 4.9 copy-start.6
  1365.6 3.5 copy-start.25
  1365.8 3.9 copy-start.22
  1369.2 2.0 copy-start.4
  1369.2 2.0 copy-start.12
  1369.8 5.8 copy-start.23
  1371.2 3.6 copy-start.27
  1371.2 3.7 copy-start.18
  1374.8 1.2 copy-start.33
  1376.0 4.6 copy-start.10
  1448.7 857.9 %all-reduce.14.cloned.1.call-start = ((), (), s32[]{:S(2)}) async-start(), calls=%async_computation.11 | async-start | bytes 23396352 | tf_op jit(solution)/shard_map/psum | solution.py:342
  2078.4 2.1 copy-start.8
  2104.5 2.6 copy-start.34
  2311.2 9.2 copy-start.19
  (5 other events, 4.8 us)
Sparse Core Ops, SparseCore 0:
  9.6 67.9 all-gather.8
  84.0 22.0 all-gather.10
  108.0 60.8 all-gather.12
  170.3 51.1 all-gather.14
  223.1 237.9 all-gather.16
  462.5 237.3 all-gather.18
  701.6 237.3 all-gather.20
  974.1 267.4 reduce-scatter.4
  1448.8 629.5 reduce-scatter.2
  2082.0 224.5 all-reduce.13
where the time goes:
time: 2340 us; the launch traced here: 2330 us
  waiting for transfers between devices  1540 us (66%)
  matrix products  274 us (12%)
  blocking collectives  242 us (10%)
  local copies, waits for them, and re-layouts  128 us (5%)
  other arithmetic  118 us (5%)
    reduce_scatter x1, waiting for transfers between devices, shards(): lax.psum_scatter(jnp.concatenate([lax.dot_general(normed_two, grad_gate_u...  630 us
    all_gather x1, waiting for transfers between devices, shards(): lax.all_gather(w_down, 'fsdp', axis=0, tiled=True)  223 us
    all_gather x1, waiting for transfers between devices, shards(): lax.all_gather(w_up, 'fsdp', axis=0, tiled=True)  223 us
    unnamed x3, blocking collectives  218 us
    all_gather x1, waiting for transfers between devices, shards(): lax.all_gather(w_gate, 'fsdp', axis=0, tiled=True)  204 us
    psum x1, waiting for transfers between devices, shards(): lax.psum(weight_rows.astype(jnp.bfloat16), 'ctx').astype(jnp.float32)  161 us
  transfers between devices with their start and end apart: 10, of which 8 were waited for; matrix products, arithmetic and copies ran while one was open for 20% of the time, Pallas kernels for 0%

commit v1 on v0

--- a/solution.py
+++ b/solution.py
@@ -339,7 +339,9 @@
         lax.psum_scatter(grad_bias_value, "fsdp", scatter_dimension=0, tiled=True),
     )
     weight_rows, down_rows, gain_one_rows, gain_two_rows, bias_rows, value_bias_rows = (
-        lax.psum(weight_rows.astype(jnp.bfloat16), "ctx").astype(jnp.float32),
+        jnp.sum(lax.all_gather(weight_rows.astype(jnp.bfloat16), "ctx"), axis=0).astype(
+            jnp.float32
+        ),
         lax.psum(down_rows.astype(jnp.bfloat16), "ctx").astype(jnp.float32),
         lax.psum(gain_one_rows.astype(jnp.bfloat16), "ctx").astype(jnp.float32),
         lax.psum(gain_two_rows.astype(jnp.bfloat16), "ctx").astype(jnp.float32),

time: 2340 us -> 2510 us (1.073)
  waiting for transfers between devices: 1540 us -> 1690 us
    all_gather x0 -> x1, waiting for transfers between devices: none -> 289 us  [shards(): lax.all_gather(weight_rows.astype(jnp.bfloat16), 'ctx')]
    psum x1, waiting for transfers between devices: 161 us -> 26.4 us  [shards(): lax.psum(down_rows.astype(jnp.bfloat16), 'ctx').astype(jnp.float32)]
  transfers between devices with their start and end apart: 10 -> 11, of which waited for: 8 -> 9; matrix products, arithmetic and copies ran while one was open for 20% -> 19% of each run, Pallas kernels for 0% -> 0%
where the time goes in v1:
time: 2510 us; the launch traced here: 2500 us
  waiting for transfers between devices  1690 us (67%)
  matrix products  274 us (11%)
  blocking collectives  243 us (10%)
  other arithmetic  136 us (5%)
  local copies, waits for them, and re-layouts  128 us (5%)
    reduce_scatter x1, waiting for transfers between devices, shards(): lax.psum_scatter(jnp.concatenate([lax.dot_general(normed_two, grad_gate_u...  628 us
    all_gather x1, waiting for transfers between devices, shards(): lax.all_gather(weight_rows.astype(jnp.bfloat16), 'ctx')  289 us
    all_gather x1, waiting for transfers between devices, shards(): lax.all_gather(w_down, 'fsdp', axis=0, tiled=True)  223 us
    all_gather x1, waiting for transfers between devices, shards(): lax.all_gather(w_up, 'fsdp', axis=0, tiled=True)  223 us
    unnamed x3, blocking collectives  219 us
    all_gather x1, waiting for transfers between devices, shards(): lax.all_gather(w_gate, 'fsdp', axis=0, tiled=True)  204 us
  transfers between devices with their start and end apart: 11, of which 9 were waited for; matrix products, arithmetic and copies ran while one was open for 19% of the time, Pallas kernels for 0%

profile of v1, /device:TPU:0, one launch (start us, length us, event | category | flops | bytes accessed | tf_op | source)
XLA Modules:
  0.0 2503.3 jit_solution(18057243863386814175)
XLA Ops:
  9.8 13.5 all-gather.1
  27.0 15.6 all-reduce.8
  46.4 31.2 %all-gather.11.cloned.1.call-done = bf16[1536,2048]{1,0:T(8,128)(2,1)} async-done(((bf16[192,2048]{1,0:T(8,128)(2,1)}), bf16[1536,2048]{1,0:T(8,128)(2,1)}) %all-gather.11.cloned.1.call-update) | async-done | bytes 6291472 | tf_op jit(solution)/shard_map/all_gather | solution.py:122
  77.6 4.0 convolution_add_fusion.4
  84.0 22.2 all-gather.13.cloned.1.call-done
  125.7 43.1 %all-gather.15.cloned.1.call-done = bf16[1280,4,512]{2,1,0:T(4,128)(2,1)} async-done(((bf16[320,4,512]{2,1,0:T(4,128)(2,1)}), bf16[1280,4,512]{2,1,0:T(4,128)(2,1)}) %all-gather.15.cloned.1.call-update) | async-done | bytes 5242896 | tf_op jit(solution)/shard_map/all_gather | solution.py:175
  168.8 82.5 %while.34 = (s32[]{:T(128)}, f32[2,2,480]{2,1,0:T(2,128)S(1)}, f32[2,2,480]{2,1,0:T(2,128)S(1)}, f32[2,2,480,128]{3,2,1,0:T(8,128)}, s32[5]{0:T(128)S(1)}, /*ind...) while((s32[]{:T(128)}, f32[2,2,480]{2,1,0:T(2,128)S(1)}, ...), condition=%wide.region_6.7_spmd.clone, body=%wide.region_2.6_spmd.clone.sunk | while | flops 514415264 | bytes 27955316 | solution.py:194
  180.6 4.4 fusion.146
  196.7 4.7 fusion.146
  213.0 4.7 fusion.146
  229.2 5.5 fusion.146
  246.4 4.7 fusion.146
  257.4 203.6 %all-gather.19.cloned.1.call-done = bf16[1536,8960]{1,0:T(8,128)(2,1)} async-done(((bf16[192,8960]{1,0:T(8,128)(2,1)}), bf16[1536,8960]{1,0:T(8,128)(2,1)}) %all-gather.19.cloned.1.call-update) | async-done | bytes 27525136 | tf_op jit(solution)/shard_map/all_gather | solution.py:203
  461.0 16.3 fusion.69
  477.3 222.6 %all-gather.21.cloned.1.call-done = bf16[1536,8960]{1,0:T(8,128)(2,1)} async-done(((bf16[192,8960]{1,0:T(8,128)(2,1)}), bf16[1536,8960]{1,0:T(8,128)(2,1)}) %all-gather.21.cloned.1.call-update) | async-done | bytes 27525136 | tf_op jit(solution)/shard_map/all_gather | solution.py:204
  699.9 16.4 fusion.70
  716.4 222.6 %all-gather.23.cloned.1.call-done = bf16[8960,1536]{1,0:T(8,128)(2,1)} async-done(((bf16[1120,1536]{1,0:T(8,128)(2,1)}), bf16[8960,1536]{1,0:T(8,128)(2,1)}) %all-gather.23.cloned.1.call-update) | async-done | bytes 27525136 | tf_op jit(solution)/shard_map/all_gather | solution.py:205
  939.0 19.8 multiply_convert_fusion
  958.8 15.2 convolution_convert_fusion.1
  974.1 17.0 fusion.71
  991.1 16.1 multiply_reduce_fusion
  1008.4 4.1 convolution_convert_fusion.4
  1014.9 4.9 broadcast_in_dim.152
  1019.8 165.6 %while.35 = (s32[]{:T(128)}, f32[2,2,480,128]{3,2,1,0:T(8,128)}, f32[1280,4,512]{2,1,0:T(4,128)}, s32[5]{0:T(128)S(1)}, s32[2,8]{1,0:T(2,128)S(1)}, /*index=5*/b...) while((s32[]{:T(128)}, f32[2,2,480,128]{3,2,1,0:T(8,128)}, ...), condition=%wide.region_12.13_spmd.clone, body=%wide.region_10.12_spmd.clone.sunk | while | flops 1270183168 | bytes 55970532 | solution.py:283
  1028.0 4.0 fusion.160
  1035.6 3.8 fusion.161
  1060.0 4.0 fusion.160
  1068.8 3.8 fusion.161
  1093.1 3.9 fusion.160
  1101.9 4.2 fusion.161
  1126.7 3.9 fusion.160
  1135.6 3.9 fusion.161
  1160.0 3.9 fusion.160
  1168.8 3.8 fusion.161
  1188.3 177.0 %all-reduce.14 = bf16[1280,4,512]{2,1,0:T(4,128)(2,1)} all-reduce(f32[1280,4,512]{2,1,0:T(4,128)} %get-tuple-element.344), channel_id=3, replica_groups=mesh['ctx'=4,'fsdp'=8] {'ctx','fsdp'}, use_global_device_ids=true, to_apply=%region_13.14.clone | all-reduce | flops 2621440 | bytes 15728640
  1376.7 4.6 convolution_convert_fusion.2
  1381.3 23.8 convolution_convert_fusion
  1405.1 44.4 %pad_maximum_fusion = bf16[1536,21504]{1,0:T(8,128)(2,1)} fusion(bf16[1536,1536]{1,0:T(8,128)(2,1)} %convolution_convert_fusion.3, bf16[1536,2048]{1,0:T(8,128)(2,1)} %convolution_convert_fusion.2, bf16[1536,17920]{1,0:T(8,128)(2,1)} %convolution_convert_fusion), kind=kLoop, calls=%fused_computation.73 | loop fusion | flops 198180864 | bytes 132120576 | tf_op jit(solution)/shard_map/concatenate | solution.py:306
  1450.1 628.3 %reduce-scatter.3.cloned.1.call-done = bf16[192,21504]{1,0:T(8,128)(2,1)} async-done(((bf16[1536,21504]{1,0:T(8,128)(2,1)}), bf16[192,21504]{1,0:T(8,128)(2,1)}) %reduce-scatter.3.cloned.1.call-update) | async-done | bytes 8257552 | tf_op jit(solution)/shard_map/reduce_scatter | solution.py:305
  2080.5 16.2 fusion.44
  2098.6 5.2 multiply_reduce_fusion.1
  2106.5 26.1 %all-reduce.7 = (bf16[1536]{0:T(1024)(128)(2,1)S(1)}, bf16[1792]{0:T(1024)(128)(2,1)S(1)}, bf16[256]{0:T(256)(128)(2,1)S(1)}, bf16[1536]{0:T(1024)(128)(2,1)S(1)}) all-reduce(f32[1536]{0:T(1024)S(1)} %get-tuple-element.419, f32[1792]{0:T(1024)S(1)} %bitcast.255, ...), channel_id=4, replica_groups=mesh['ctx'=4,'fsdp'=8] {'fsdp'}, use_global_device_ids=true, to_apply=%region_16.17.clone | all-reduce | flops 5120 | bytes 30720
  2132.8 10.6 all-reduce.9
  2145.7 26.4 %all-reduce.13.cloned.1.call-done = bf16[1120,1536]{1,0:T(8,128)(2,1)} async-done(((bf16[1120,1536]{1,0:T(8,128)(2,1)}), bf16[1120,1536]{1,0:T(8,128)(2,1)}) %all-reduce.13.cloned.1.call-update) | async-done | bytes 3440656 | tf_op jit(solution)/shard_map/psum | solution.py:345
  2172.1 5.8 convert_element_type.186
  2177.9 288.8 %all-gather.25.cloned.1.call-done = bf16[768,21504]{1,0:T(8,128)(2,1)} async-done(((bf16[192,21504]{1,0:T(8,128)(2,1)}), bf16[768,21504]{1,0:T(8,128)(2,1)}) %all-gather.25.cloned.1.call-update) | async-done | bytes 33030160 | tf_op jit(solution)/shard_map/all_gather | solution.py:342
  2466.7 16.1 reduce_sum.139
  2487.4 9.1 fusion.62
  (490 shorter events, 240.0 us)
Async XLA Ops:
  7.2 70.4 %all-gather.11.cloned.1.call-start = ((), (), s32[]{:S(2)}) async-start(), calls=%async_computation.2 | async-start | bytes 7077888 | tf_op jit(solution)/shard_map/all_gather | solution.py:122
  7.9 98.2 %all-gather.13.cloned.1.call-start = ((), (), s32[]{:S(2)}) async-start(), calls=%async_computation.3 | async-start | bytes 1474560 | tf_op jit(solution)/shard_map/all_gather | solution.py:150
  9.1 72.6 %copy-start = (f32[160,1536]{1,0:T(8,128)}, f32[160,1536]{1,0:T(8,128)S(1)}, u32[]{:S(2)}) copy-start(f32[160,1536]{1,0:T(8,128)S(1)} %reshape.608) | copy-start | bytes 2949124
  42.6 39.1 %copy-start.28 = (f32[1536]{0:T(1024)}, f32[1536]{0:T(1024)S(1)}, u32[]{:S(2)}) copy-start(f32[1536]{0:T(1024)S(1)} %convert_element_type.153) | copy-start | bytes 18436
  44.1 33.6 %copy-start.31 = (f32[160]{0:T(256)}, f32[160]{0:T(256)S(1)}, u32[]{:S(2)}) copy-start(f32[160]{0:T(256)S(1)} %rsqrt.20) | copy-start | bytes 1924
  45.6 36.7 %copy-start.25 = (f32[160,128]{1,0:T(8,128)}, f32[160,128]{1,0:T(8,128)S(1)}, u32[]{:S(2)}) copy-start(f32[160,128]{1,0:T(8,128)S(1)} %pad_maximum_fusion.4) | copy-start | bytes 245764
  46.4 35.7 %copy-start.23 = (f32[160,128]{1,0:T(8,128)}, f32[160,128]{1,0:T(8,128)S(1)}, u32[]{:S(2)}) copy-start(f32[160,128]{1,0:T(8,128)S(1)} %get-tuple-element.499) | copy-start | bytes 245764
  81.7 25.7 %copy-start.13 = (f32[160,2048]{1,0:T(8,128)}, f32[160,2048]{1,0:T(8,128)S(1)}, u32[]{:S(2)}) copy-start(f32[160,2048]{1,0:T(8,128)S(1)} %convolution_add_fusion.4) | copy-start | bytes 3932164
  83.9 84.9 %all-gather.15.cloned.1.call-start = ((), (), s32[]{:S(2)}) async-start(), calls=%async_computation.4 | async-start | bytes 6553600 | tf_op jit(solution)/shard_map/all_gather | solution.py:175
  106.1 147.5 %all-gather.17.cloned.1.call-start = ((), (), s32[]{:S(2)}) async-start(), calls=%async_computation.5 | async-start | bytes 5308416 | tf_op jit(solution)/shard_map/all_gather | solution.py:123
  106.7 354.3 %all-gather.19.cloned.1.call-start = ((), (), s32[]{:S(2)}) async-start(), calls=%async_computation.6 | async-start | bytes 30965760 | tf_op jit(solution)/shard_map/all_gather | solution.py:203
  107.3 1.9 copy-start.27
  107.3 592.6 %all-gather.21.cloned.1.call-start = ((), (), s32[]{:S(2)}) async-start(), calls=%async_computation.7 | async-start | bytes 30965760 | tf_op jit(solution)/shard_map/all_gather | solution.py:204
  107.4 5.0 copy-start.14
  107.9 831.1 %all-gather.23.cloned.1.call-start = ((), (), s32[]{:S(2)}) async-start(), calls=%async_computation.8 | async-start | bytes 30965760 | tf_op jit(solution)/shard_map/all_gather | solution.py:205
  108.7 1340.9 %reduce-scatter.5.cloned.1.call-start = ((), (), s32[]{:S(2)}) async-start(), calls=%async_computation.10 | async-start | bytes 30965760 | tf_op jit(solution)/shard_map/reduce_scatter | solution.py:327
  116.4 7.4 copy-start.15
  122.0 46.8 %copy-start.30 = (s32[2,8]{1,0:T(2,128)S(1)}, s32[2,8]{1,0:T(2,128)}, u32[]{:S(2)}) copy-start(s32[2,8]{1,0:T(2,128)} %param.16) | copy-start | bytes 196
  251.3 2.4 copy-start.1
  253.7 3.8 copy-start.11
  257.2 750.0 %copy-start.7 = (f32[160,1536]{1,0:T(8,128)}, f32[160,1536]{1,0:T(8,128)S(1)}, u32[]{:S(2)}) copy-start(f32[160,1536]{1,0:T(8,128)S(1)} %get-tuple-element.511) | copy-start | bytes 2949124
  257.4 442.5 %copy-start.9 = (bf16[160,1536]{1,0:T(8,128)(2,1)}, bf16[160,1536]{1,0:T(8,128)(2,1)S(1)}, u32[]{:S(2)}) copy-start(bf16[160,1536]{1,0:T(8,128)(2,1)S(1)} %multiply_convert_fusion.3) | copy-start | bytes 1474564
  477.3 461.7 %copy-start.16 = (bf16[160,1536]{1,0:T(8,128)(2,1)S(1)}, bf16[160,1536]{1,0:T(8,128)(2,1)}, u32[]{:S(2)}) copy-start(bf16[160,1536]{1,0:T(8,128)(2,1)} %reshape.600) | copy-start | bytes 1474564
  974.0 1104.4 %reduce-scatter.3.cloned.1.call-start = ((), (), s32[]{:S(2)}) async-start(), calls=%async_computation.9 | async-start | bytes 74317824 | tf_op jit(solution)/shard_map/reduce_scatter | solution.py:305
  1008.4 5.8 copy-start.17
  1028.0 4.0 copy-start.5
  1032.0 3.6 copy-start.6
  1060.0 4.0 copy-start.5
  1064.0 4.9 copy-start.6
  1093.1 3.9 copy-start.5
  1097.1 4.9 copy-start.6
  1126.7 3.9 copy-start.5
  1130.6 4.9 copy-start.6
  1160.0 3.9 copy-start.5
  1163.9 4.9 copy-start.6
  1366.3 3.5 copy-start.24
  1366.4 3.9 copy-start.21
  1369.8 2.0 copy-start.4
  1369.8 2.0 copy-start.12
  1370.4 5.8 copy-start.22
  1371.8 3.6 copy-start.26
  1371.8 3.7 copy-start.18
  1375.5 1.2 copy-start.32
  1376.7 4.6 copy-start.10
  1449.5 722.6 %all-reduce.13.cloned.1.call-start = ((), (), s32[]{:S(2)}) async-start(), calls=%async_computation.11 | async-start | bytes 6881280 | tf_op jit(solution)/shard_map/psum | solution.py:345
  1450.1 1016.6 %all-gather.25.cloned.1.call-start = ((), (), s32[]{:S(2)}) async-start(), calls=%async_computation.12 | async-start | bytes 41287680 | tf_op jit(solution)/shard_map/all_gather | solution.py:342
  2078.4 2.1 copy-start.8
  2103.9 2.6 copy-start.33
  (5 other events, 4.8 us)
Sparse Core Ops, SparseCore 0:
  9.6 67.9 all-gather.10
  84.0 22.0 all-gather.12
  108.0 60.8 all-gather.14
  170.3 51.1 all-gather.16
  223.1 237.9 all-gather.18
  462.5 237.3 all-gather.20
  701.6 237.3 all-gather.22
  974.1 267.4 reduce-scatter.4
  1449.6 628.7 reduce-scatter.2
  2081.5 90.5 all-reduce.12
  2174.0 292.7 all-gather.24
